TPU v7x, 8 devices: a whole 2x2x1 slice. The times are simulated.
8 devices in a mesh: dp: 2 (over z, y), tp: 4 (over x, core).
Axes of the slice: x: 2, y: 2, z: 1, core: 2. Of those that a mesh axis runs over, the one named last changes fastest.
Arguments:
- token_ids: int32 [128], P('dp'), parts along dimension 0
- embed_table: bfloat16 [32768, 4096], P('tp')
- norm_gain: bfloat16 [4096], replicated
- w_in: bfloat16 [4096, 14336], P(None, 'tp')
- w_out: bfloat16 [14336, 4096], P('tp')
Outputs:
- output: bfloat16 [128, 4096], P(('dp', 'tp')), parts along dimension 0
There are 2 independent parts. A program takes and returns all parts, laid end to end along the dimension named above; an argument that names none is the same for every part.
All inputs are finite; a program needn't handle non-finite values.
Results may differ from a plain program's by a relative error of at most 0.00789354.
Values are sent between devices in bfloat16 or wider.
A program may use at most 1 GiB of HBM per device.

v0:
```python
import jax
import jax.numpy as jnp
from jax import lax
from jax.sharding import PartitionSpec as P

RMS_EPS = 1e-6


def rms_norm(row_vals, norm_gain):
    rows_f32 = row_vals.astype(jnp.float32)
    inv_rms = lax.rsqrt(jnp.mean(rows_f32 * rows_f32, axis=-1, keepdims=True) + RMS_EPS)
    return (rows_f32 * inv_rms * norm_gain.astype(jnp.float32)).astype(jnp.bfloat16)


def solution(mesh):
    def device_step(token_ids, table_shard, norm_gain, w_in_shard, w_out_shard):
        shard_rows = table_shard.shape[0]
        row_offset = lax.axis_index("tp") * shard_rows
        local_ids = token_ids - row_offset
        owned = (local_ids >= 0) & (local_ids < shard_rows)
        looked_up = jnp.take(table_shard, jnp.clip(local_ids, 0, shard_rows - 1), axis=0, mode="clip")
        partial_rows = jnp.where(owned[:, None], looked_up, jnp.zeros((), jnp.bfloat16))
        embedded = lax.psum_scatter(partial_rows, "tp", scatter_dimension=0, tiled=True)
        normed = rms_norm(embedded, norm_gain)
        normed_all = lax.all_gather(normed, "tp", axis=0, tiled=True)
        pre_act = jnp.dot(normed_all, w_in_shard, preferred_element_type=jnp.float32).astype(jnp.bfloat16)
        activated = jax.nn.gelu(pre_act.astype(jnp.float32), approximate=True).astype(jnp.bfloat16)
        mlp_part = jnp.dot(activated, w_out_shard, preferred_element_type=jnp.float32)
        mlp_sum = lax.psum_scatter(mlp_part, "tp", scatter_dimension=0, tiled=True)
        return (embedded.astype(jnp.float32) + mlp_sum).astype(jnp.bfloat16)

    return jax.shard_map(
        device_step,
        mesh=mesh,
        in_specs=(P("dp"), P("tp", None), P(), P(None, "tp"), P("tp", None)),
        out_specs=P(("dp", "tp"), None),
        check_vma=False,
    )
```

profile of v0, /device:TPU:0, one launch (start us, length us, event | category | flops | bytes accessed | tf_op | source)
XLA Modules:
  0.0 94.6 jit_solution(13470747054259438482)
XLA Ops:
  6.5 0.0 reduce-scatter.3.cloned.1.call-start
  6.5 0.7 compare_and_fusion
  7.2 0.7 subtract_clamp_fusion
  7.9 3.7 %gather_fusion = bf16[64,4096]{1,0:T(8,128)(2,1)S(1)} fusion(bf16[8192,4096]{1,0:T(8,128)(2,1)} %param.6, s32[1024]{0:T(1024)S(1)} %pad_clamp_fusion), kind=kCustom, calls=%fused_computation | custom fusion | bytes 1048832 | tf_op jit(solution)/shard_map/jit(_take)/gather | solution.py:21
  11.6 0.9 broadcast_select_fusion
  12.5 0.0 reduce-scatter.3.cloned.1.call-update
  12.5 0.0 reduce-scatter.5.cloned.1.call-start
  12.6 0.7 convert_element_type.23
  13.3 18.3 %reduce-scatter.3.cloned.1.call-done = bf16[16,4096]{1,0:T(8,128)(2,1)} async-done(((bf16[64,4096]{1,0:T(8,128)(2,1)}), bf16[16,4096]{1,0:T(8,128)(2,1)}) %reduce-scatter.3.cloned.1.call-update) | async-done | bytes 131088 | tf_op jit(solution)/shard_map/reduce_scatter | solution.py:23
  31.6 1.0 %fusion.14 = f32[16]{0:T(128)S(1)} fusion(bf16[16,4096]{1,0:T(8,128)(2,1)} %reduce-scatter.3.cloned.1.call-done), kind=kLoop, calls=%fused_computation.21 | loop fusion | flops 196592 | bytes 131136 | tf_op jit(solution)/shard_map/reduce_sum | solution.py:11
  32.7 1.0 %fusion.16 = bf16[16,4096]{1,0:T(8,128)(2,1)S(1)} fusion(bf16[16,4096]{1,0:T(8,128)(2,1)} %reduce-scatter.3.cloned.1.call-done, f32[4096]{0:T(1024)S(1)} %convert_element_type.23, f32[16]{0:T(128)S(1)} %add_rsqrt_fusion), kind=kLoop, calls=%fused_computation.23 | loop fusion | flops 262144 | bytes 278592 | tf_op jit(solution)/shard_map/convert_element_type | solution.py:12
  33.7 9.3 %all_gather.3 = bf16[64,4096]{1,0:T(8,128)(2,1)S(1)} all-gather(bf16[16,4096]{1,0:T(8,128)(2,1)S(1)} %fusion.16), channel_id=1, replica_groups=mesh['dp'=2,'tp'=4] {'tp'}, dimensions={0}, use_global_device_ids=true | all-gather | bytes 655360 | tf_op jit(solution)/shard_map/all_gather | solution.py:25
  43.0 0.0 copy-start
  43.0 23.1 %fusion.9 = f32[64,4096]{1,0:T(8,128)} fusion(bf16[3584,4096]{1,0:T(8,128)(2,1)} %param.9, bf16[64,4096]{1,0:T(8,128)(2,1)S(1)} %all_gather.3, bf16[4096,3584]{1,0:T(8,128)(2,1)} %param.8), kind=kOutput, calls=%fused_computation.12 | convolution fusion | flops 3760619520 | bytes 60293120 | tf_op jit(solution)/shard_map/dot_general | solution.py:28
  66.1 0.0 reduce-scatter.5.cloned.1.call-update
  66.1 20.0 %reduce-scatter.5.cloned.1.call-done = f32[16,4096]{1,0:T(8,128)} async-done(((f32[64,4096]{1,0:T(8,128)}), f32[16,4096]{1,0:T(8,128)}) %reduce-scatter.5.cloned.1.call-update) | async-done | bytes 262160 | tf_op jit(solution)/shard_map/reduce_scatter | solution.py:29
  86.1 0.0 copy-done
  86.1 1.6 %fusion.17 = bf16[16,4096]{1,0:T(8,128)(2,1)} fusion(f32[16,4096]{1,0:T(8,128)} %reduce-scatter.5.cloned.1.call-done, bf16[16,4096]{1,0:T(8,128)(2,1)S(1)} %copy-done), kind=kLoop, calls=%fused_computation.24 | loop fusion | flops 196608 | bytes 524288 | tf_op jit(solution)/shard_map/convert_element_type | solution.py:30
  (2 shorter events, 0.0 us)
Async XLA Ops:
  6.5 25.1 %reduce-scatter.3.cloned.1.call-start = ((), (), s32[]{:S(2)}) async-start(), calls=%async_computation.2 | async-start | bytes 655360 | tf_op jit(solution)/shard_map/reduce_scatter | solution.py:23
  12.5 73.6 %reduce-scatter.5.cloned.1.call-start = ((), (), s32[]{:S(2)}) async-start(), calls=%async_computation.3 | async-start | bytes 1310720 | tf_op jit(solution)/shard_map/reduce_scatter | solution.py:29
  43.0 43.2 %copy-start = (bf16[16,4096]{1,0:T(8,128)(2,1)S(1)}, bf16[16,4096]{1,0:T(8,128)(2,1)}, u32[]{:S(2)}) copy-start(bf16[16,4096]{1,0:T(8,128)(2,1)} %reduce-scatter.3.cloned.1.call-done) | copy-start | bytes 393220
Sparse Core Ops, SparseCore 0:
  12.6 18.9 reduce-scatter.2
  66.3 19.8 reduce-scatter.4
where the time goes:
time: 95.1 us; the launch traced here: 94.6 us
  waiting for transfers between devices  38.4 us (40%)
  matrix products  23.1 us (24%)
  between operations  13.4 us (14%)
  blocking collectives  9.3 us (10%)
  other arithmetic  6.62 us (7%)
  local copies, waits for them, and re-layouts  3.72 us (4%)
    dot_general x1, matrix products, device_step(): jnp.dot(activated, w_out_shard, preferred_element_type=jnp.float32)  23.1 us
    reduce_scatter x1, waiting for transfers between devices, device_step(): mlp_sum = lax.psum_scatter(mlp_part, 'tp', scatter_dimension=0, tiled=True)  20 us
    reduce_scatter x1, waiting for transfers between devices, device_step(): lax.psum_scatter(partial_rows, 'tp', scatter_dimension=0, tiled=True)  18.3 us
    all_gather x1, blocking collectives, device_step(): normed_all = lax.all_gather(normed, 'tp', axis=0, tiled=True)  9.3 us
    gather x1, local copies, waits for them, and re-layouts, device_step(): jnp.take(table_shard, jnp.clip(local_ids, 0, shard_rows - 1), axis=0, mod...  3.72 us
  transfers between devices with their start and end apart: 2, of which 2 were waited for; matrix products, arithmetic and copies ran while one was open for 1% of the time, Pallas kernels for 0%

commit v1 on v0

v1 whole, which is shorter than its diff:
```python
import jax
import jax.numpy as jnp
from jax import lax
from jax.experimental import pallas as pl
from jax.experimental.pallas import tpu as pltpu
from jax.sharding import PartitionSpec as P

RMS_EPS = 1e-6
MESH = pl.DeviceIdType.MESH
KC = 512
NC = 512


def gather_kernel(ids_ref, table_ref, gain_ref, n_ref, x_ref, buf, tgt, sem):
    tokens = ids_ref.shape[0]
    blocks = table_ref.shape[0]
    dim = table_ref.shape[2]
    first = lax.axis_index("tp") * (blocks * 8)
    for i in range(tokens):
        local = ids_ref[i] - first
        owned = (local >= 0) & (local < blocks * 8)

        @pl.when(owned)
        def _():
            pltpu.make_async_copy(
                table_ref.at[lax.shift_right_logical(local, 3)], buf.at[i], sem.at[i]
            ).start()

        @pl.when(jnp.logical_not(owned))
        def _():
            buf[i] = jnp.zeros(buf.shape[1:], buf.dtype)

        tgt[i, :] = jnp.full((128,), jnp.where(owned, i * 8 + (local & 7), -1), jnp.int32)
    for i in range(tokens):
        local = ids_ref[i] - first
        owned = (local >= 0) & (local < blocks * 8)

        @pl.when(owned)
        def _():
            pltpu.make_async_copy(table_ref.at[0], buf.at[i], sem.at[i]).wait()

    lane = lax.broadcasted_iota(jnp.int32, (tokens, 128), 1)
    want = tgt[...]
    pick = jnp.concatenate(
        [jnp.where(lane + 128 * b == want, 1.0, 0.0) for b in range(tokens * 8 // 128)], axis=1
    ).astype(jnp.bfloat16)
    rows = jnp.dot(
        pick, buf[...].reshape(tokens * 8, dim), preferred_element_type=jnp.float32
    )
    inv_rms = lax.rsqrt(jnp.mean(rows * rows, axis=-1, keepdims=True) + RMS_EPS)
    normed = (rows * inv_rms * gain_ref[...].astype(jnp.float32)).astype(jnp.bfloat16)
    rows = rows.astype(jnp.bfloat16)
    for g in range(dim // KC):
        n_ref[g] = normed[:, g * KC : (g + 1) * KC]
        x_ref[g] = rows[:, g * KC : (g + 1) * KC]


def block_kernel(
    n_ref, x_ref, w1_ref, w2_ref, out_ref,
    w1, w2, comb, mine, other, acc, hid, y, y_in, z, z_in,
    w1_sem, w2_sem, ps, pr, xs, xr, fs, fr, ys, yr, zs, zr,
):
    tp = lax.axis_index("tp")
    chip, core = tp // 2, tp % 2
    partner = {"tp": chip * 2 + (1 - core)}
    peer = {"tp": (1 - chip) * 2 + core}
    halves = n_ref.shape[0] // 2
    outs = w2.shape[0]
    my0, other0 = core * halves, (1 - core) * halves

    def w1_copy(g):
        return pltpu.make_async_copy(
            w1_ref.at[pl.ds(pl.multiple_of(g * KC, KC), KC), :], w1.at[g], w1_sem.at[g]
        )

    def w2_copy(m):
        return pltpu.make_async_copy(
            w2_ref.at[:, pl.ds(pl.multiple_of(m * NC, NC), NC)], w2.at[m], w2_sem.at[m]
        )

    def part_copy(j):
        return pltpu.make_async_remote_copy(
            n_ref.at[other0 + j], comb.at[j], ps.at[j], pr.at[j], partner, MESH
        )

    def peer_copy(j):
        return pltpu.make_async_remote_copy(
            comb.at[j], mine.at[j], xs.at[j], xr.at[j], peer, MESH
        )

    def full_copy(j):
        return pltpu.make_async_remote_copy(
            mine.at[j], other.at[j], fs.at[j], fr.at[j], partner, MESH
        )

    def y_copy(m):
        return pltpu.make_async_remote_copy(
            y.at[m, 1 - core], y_in.at[m], ys.at[m], yr.at[m], partner, MESH
        )

    def z_copy(m):
        return pltpu.make_async_remote_copy(
            z.at[m, 1 - chip], z_in.at[m], zs.at[m], zr.at[m], peer, MESH
        )

    barrier = pltpu.get_barrier_semaphore()
    for who in (partner, peer):
        pl.semaphore_signal(barrier, inc=1, device_id=who, device_id_type=MESH)
    for j in range(halves):
        w1_copy(my0 + j).start()
        w1_copy(other0 + j).start()
    for m in range(outs):
        w2_copy(m).start()
    pl.semaphore_wait(barrier, 2)

    for j in range(halves):
        part_copy(j).start()
    for j in range(halves):
        part_copy(j).wait_recv()
        comb[j] += n_ref[my0 + j]
        peer_copy(j).start()

    acc[...] = jnp.zeros_like(acc)

    @pl.loop(0, halves)
    def _(j):
        peer_copy(j).wait_recv()
        mine[j] += comb[j]
        full_copy(j).start()
        w1_copy(my0 + j).wait()
        acc[...] += jnp.dot(mine[j], w1[my0 + j], preferred_element_type=jnp.float32)
        full_copy(j).wait_recv()
        w1_copy(other0 + j).wait()
        acc[...] += jnp.dot(other[j], w1[other0 + j], preferred_element_type=jnp.float32)

    hid[...] = jax.nn.gelu(
        acc[...].astype(jnp.bfloat16).astype(jnp.float32), approximate=True
    ).astype(jnp.bfloat16)

    rows = out_ref.shape[0]

    def combine(m):
        y_copy(m).wait_recv()
        z[m] = y[m, core] + y_in[m]
        z_copy(m).start()

    def finish(m):
        z_copy(m).wait_recv()
        out_ref[:, pl.ds(pl.multiple_of(m * NC, NC), NC)] = (z[m, chip] + z_in[m]).astype(
            out_ref.dtype
        )

    @pl.loop(0, outs)
    def _(m):
        w2_copy(m).wait()
        total = x_ref[m].astype(jnp.float32) + jnp.dot(
            hid[...], w2[m], preferred_element_type=jnp.float32
        )
        for dest_core in range(2):
            for dest_chip in range(2):
                at = (dest_chip * 2 + dest_core) * rows
                y[m, dest_core, dest_chip] = total[at : at + rows]
        y_copy(m).start()

        @pl.when(m >= 1)
        def _():
            combine(m - 1)

    combine(outs - 1)

    @pl.loop(0, outs)
    def _(m):
        finish(m)

    for j in range(halves):
        part_copy(j).wait_send()
        peer_copy(j).wait_send()
        full_copy(j).wait_send()
    for m in range(outs):
        y_copy(m).wait_send()
        z_copy(m).wait_send()


def solution(mesh):
    def device_step(token_ids, table, gain, w_in, w_out):
        tokens = token_ids.shape[0]
        vocab, dim = table.shape
        width = w_in.shape[1]
        chunks, halves, outs = dim // KC, dim // KC // 2, dim // NC
        rows = tokens // 4
        vmem = pl.BlockSpec(memory_space=pltpu.VMEM)
        hbm = pl.BlockSpec(memory_space=pl.ANY)
        piece = jax.ShapeDtypeStruct((chunks, tokens, KC), jnp.bfloat16)
        normed, embedded = pl.pallas_call(
            gather_kernel,
            name="gather_norm",
            out_shape=(piece, piece),
            in_specs=[pl.BlockSpec(memory_space=pltpu.SMEM), hbm, vmem],
            out_specs=(vmem, vmem),
            scratch_shapes=[
                pltpu.VMEM((tokens, 8, dim), jnp.bfloat16),
                pltpu.VMEM((tokens, 128), jnp.int32),
                pltpu.SemaphoreType.DMA((tokens,)),
            ],
            compiler_params=pltpu.CompilerParams(vmem_limit_bytes=24 * 2**20),
        )(token_ids, table.reshape(vocab // 8, 8, dim), gain.reshape(1, dim))

        bf16, f32 = jnp.bfloat16, jnp.float32
        dma = pltpu.SemaphoreType.DMA
        return pl.pallas_call(
            block_kernel,
            name="mlp_block",
            out_shape=jax.ShapeDtypeStruct((rows, dim), bf16),
            in_specs=[vmem, vmem, hbm, hbm],
            out_specs=vmem,
            scratch_shapes=[
                pltpu.VMEM((chunks, KC, width), bf16),
                pltpu.VMEM((outs, width, NC), bf16),
                pltpu.VMEM((halves, tokens, KC), bf16),
                pltpu.VMEM((halves, tokens, KC), bf16),
                pltpu.VMEM((halves, tokens, KC), bf16),
                pltpu.VMEM((tokens, width), f32),
                pltpu.VMEM((tokens, width), bf16),
                pltpu.VMEM((outs, 2, 2, rows, NC), f32),
                pltpu.VMEM((outs, 2, rows, NC), f32),
                pltpu.VMEM((outs, 2, rows, NC), f32),
                pltpu.VMEM((outs, rows, NC), f32),
                dma((chunks,)), dma((outs,)),
                dma((halves,)), dma((halves,)),
                dma((halves,)), dma((halves,)),
                dma((halves,)), dma((halves,)),
                dma((outs,)), dma((outs,)),
                dma((outs,)), dma((outs,)),
            ],
            compiler_params=pltpu.CompilerParams(
                collective_id=0, has_side_effects=True, vmem_limit_bytes=67_043_328
            ),
        )(normed, embedded, w_in, w_out)

    return jax.shard_map(
        device_step,
        mesh=mesh,
        in_specs=(P("dp"), P("tp", None), P(), P(None, "tp"), P("tp", None)),
        out_specs=P(("dp", "tp"), None),
        check_vma=False,
    )
```

time: 95.1 us -> 41.9 us (0.44)
  waiting for transfers between devices: 38.4 us -> 0 us
  Pallas kernels: 0 us -> 37.1 us
  matrix products: 23.1 us -> 0 us
  between operations: 13.4 us -> 0.04 us
  blocking collectives: 9.3 us -> 0 us
  other arithmetic: 6.62 us -> 0 us
    reduce_scatter x2 -> x0, waiting for transfers between devices: 38.3 us -> none  [the longest x1 20 us: device_step(): mlp_sum = lax.psum_scatter(mlp_part, 'tp', scatter_dimension=0, tiled=True)]
    pallas_call x0 -> x2, Pallas kernels: none -> 37.1 us  [the longest x1 33.3 us: device_step(): pl.pallas_call(block_kernel, name='mlp_block', out_shape=jax.ShapeDtypeSt...]
    dot_general x1 -> x0, matrix products: 23.1 us -> none  [device_step(): jnp.dot(activated, w_out_shard, preferred_element_type=jnp.float32)]
    all_gather x1 -> x0, blocking collectives: 9.3 us -> none  [device_step(): normed_all = lax.all_gather(normed, 'tp', axis=0, tiled=True)]
    unnamed x2 -> x7, local copies, waits for them, and re-layouts: 0.01 us -> 3.78 us
    gather x1 -> x0, local copies, waits for them, and re-layouts: 3.72 us -> none  [device_step(): jnp.take(table_shard, jnp.clip(local_ids, 0, shard_rows - 1), axis=0, mod...]
    convert_element_type x3 -> x0, other arithmetic: 3.34 us -> none  [the longest x1 1.63 us: device_step(): return (embedded.astype(jnp.float32) + mlp_sum).astype(jnp.bfloat16)]
    reduce_sum x1 -> x0, other arithmetic: 1.05 us -> none  [rms_norm(): jnp.mean(rows_f32 * rows_f32, axis=-1, keepdims=True) + RMS_EPS]
  transfers between devices with their start and end apart: 2 -> 0, of which waited for: 2 -> 0; matrix products, arithmetic and copies ran while one was open for 1% -> 0% of each run, Pallas kernels for 0% -> 0%
where the time goes in v1:
time: 41.9 us; the launch traced here: 41.7 us
  Pallas kernels  37.1 us (89%)
  local copies, waits for them, and re-layouts  4.49 us (11%)
    pallas_call x1, Pallas kernels, device_step(): pl.pallas_call(block_kernel, name='mlp_block', out_shape=jax.ShapeDtypeSt...  33.3 us
    pallas_call x1, Pallas kernels, device_step(): pl.pallas_call(gather_kernel, name='gather_norm', out_shape=(piece, piece...  3.8 us
    unnamed x7, local copies, waits for them, and re-layouts  3.78 us

profile of v1, /device:TPU:0, one launch (start us, length us, event | category | flops | bytes accessed | tf_op | source)
XLA Modules:
  0.0 41.7 jit_solution(15626149407574112365)
XLA Ops:
  0.0 0.7 %reshape.7.gain_ref = bf16[1,4096]{1,0:T(2,128)(2,1)S(1)} reshape(bf16[4096]{0:T(1024)(128)(2,1)} %param.7) | data formatting | bytes 16384 | tf_op jit(solution)/shard_map/reshape | solution.py:206
  0.7 0.0 copy-start.2
  0.7 0.6 %copy-done.2 = s32[64]{0:T(128)S(1)} copy-done((s32[64]{0:T(128)S(1)}, s32[64]{0:T(128)}, u32[]{:S(2)}) %copy-start.2) | copy-done | bytes 280
  1.4 3.8 %gather_norm.1 = (bf16[8,64,512]{2,1,0:T(8,128)(2,1)S(1)}, bf16[8,64,512]{2,1,0:T(8,128)(2,1)S(1)}) custom-call(s32[64]{0:T(128)S(1)} %copy-done.2, bf16[1024,8,4096]{2,1,0:T(8,128)(2,1)} %bitcast.table_ref, bf16[1,4096]{1,0:T(2,128)(2,1)S(1)} %reshape.7.gain_ref), custom_call_target="tpu_custom_call" | custom-call | tf_op jit(solution)/shard_map/gather_norm/pallas_call | solution.py:194
  5.2 0.0 copy-start
  5.2 0.8 %copy-done = bf16[8,64,512]{2,1,0:T(8,128)(2,1)} copy-done((bf16[8,64,512]{2,1,0:T(8,128)(2,1)}, bf16[8,64,512]{2,1,0:T(8,128)(2,1)S(1)}, u32[]{:S(2)}) %copy-start) | copy-done | bytes 524312
  6.0 0.0 copy-start.1
  6.0 0.8 %copy-done.1 = bf16[8,64,512]{2,1,0:T(8,128)(2,1)} copy-done((bf16[8,64,512]{2,1,0:T(8,128)(2,1)}, bf16[8,64,512]{2,1,0:T(8,128)(2,1)S(1)}, u32[]{:S(2)}) %copy-start.1) | copy-done | bytes 524312
  6.8 33.3 %mlp_block.1 = bf16[16,4096]{1,0:T(8,128)(2,1)} custom-call(bf16[8,64,512]{2,1,0:T(8,128)(2,1)} %copy-done, bf16[8,64,512]{2,1,0:T(8,128)(2,1)} %copy-done.1, bf16[4096,3584]{1,0:T(8,128)(2,1)} %w1_ref.1, bf16[3584,4096]{1,0:T(8,128)(2,1)} %w2_ref.1), custom_call_target="tpu_custom_call" | custom-call | tf_op jit(solution)/shard_map/mlp_block/pallas_call | solution.py:210
  40.1 1.6 %copy.7 = bf16[16,4096]{1,0:T(8,128)(2,1)} copy(bf16[16,4096]{1,0:T(8,128)(2,1)} %mlp_block.1) | data formatting | bytes 262144
Async XLA Ops:
  0.7 0.7 %copy-start.2 = (s32[64]{0:T(128)S(1)}, s32[64]{0:T(128)}, u32[]{:S(2)}) copy-start(s32[64]{0:T(128)} %ids_ref.1) | copy-start | bytes 772
  5.2 0.8 %copy-start = (bf16[8,64,512]{2,1,0:T(8,128)(2,1)}, bf16[8,64,512]{2,1,0:T(8,128)(2,1)S(1)}, u32[]{:S(2)}) copy-start(bf16[8,64,512]{2,1,0:T(8,128)(2,1)S(1)} %get-tuple-element.7.n_ref) | copy-start | bytes 1572868
  6.0 0.8 %copy-start.1 = (bf16[8,64,512]{2,1,0:T(8,128)(2,1)}, bf16[8,64,512]{2,1,0:T(8,128)(2,1)S(1)}, u32[]{:S(2)}) copy-start(bf16[8,64,512]{2,1,0:T(8,128)(2,1)S(1)} %get-tuple-element.8.x_ref) | copy-start | bytes 1572868

commit v2 on v0

v2 whole, which is shorter than its diff:
```python
import jax
import jax.numpy as jnp
from jax import lax
from jax.experimental import pallas as pl
from jax.experimental.pallas import tpu as pltpu
from jax.sharding import PartitionSpec as P

RMS_EPS = 1e-6
MESH = pl.DeviceIdType.MESH
SUB = 8


def spans(widths):
    return [(sum(widths[:i]), w) for i, w in enumerate(widths)]


ROW_CHUNKS = spans([256, 512, 512, 512, 256])
OUT_CHUNKS = spans([256] + [512] * 7 + [256])
W1_ROWS = 3072
W2_SLOTS = 7
IN_FLIGHT = 22_100_000


def gather_kernel(ids_hbm, table_ref, gain_hbm, n_ref, x_ref, ids, gain, buf, tgt, id_sem, g_sem, sem):
    tokens, dim = x_ref.shape
    blocks = table_ref.shape[0]
    first = lax.axis_index("tp") * (blocks * SUB)
    id_copy = pltpu.make_async_copy(ids_hbm, ids, id_sem)
    id_copy.start()
    gain_copy = pltpu.make_async_copy(gain_hbm, gain, g_sem)
    gain_copy.start()
    id_copy.wait()

    def local(i):
        at = ids[i] - first
        return at, (at >= 0) & (at < blocks * SUB)

    for i in range(tokens):
        at, owned = local(i)

        @pl.when(owned)
        def _():
            pltpu.make_async_copy(
                table_ref.at[lax.shift_right_logical(at, 3)], buf.at[i], sem.at[i]
            ).start()

    for i in range(tokens):
        at, owned = local(i)

        @pl.when(jnp.logical_not(owned))
        def _():
            buf[i] = jnp.zeros(buf.shape[1:], buf.dtype)

        tgt[i, :] = jnp.full((128,), jnp.where(owned, i * SUB + (at & (SUB - 1)), -1), jnp.int32)

    lane = lax.broadcasted_iota(jnp.int32, (tokens, 128), 1)
    want = tgt[...]
    pick = jnp.concatenate(
        [jnp.where(lane + 128 * b == want, 1.0, 0.0) for b in range(tokens * SUB // 128)], axis=1
    ).astype(jnp.bfloat16)
    gain_copy.wait()
    for i in range(tokens):
        at, owned = local(i)

        @pl.when(owned)
        def _():
            pltpu.make_async_copy(table_ref.at[0], buf.at[i], sem.at[i]).wait()

    rows = jnp.dot(
        pick, buf[...].reshape(tokens * SUB, dim), preferred_element_type=jnp.float32
    )
    x_ref[...] = rows.astype(jnp.bfloat16)
    inv_rms = lax.rsqrt(jnp.mean(rows * rows, axis=-1, keepdims=True) + RMS_EPS)
    scale = gain[...].astype(jnp.float32).reshape(1, dim)
    normed = (rows * inv_rms * scale).astype(jnp.bfloat16)
    for half in range(2):
        n_ref[half] = normed[:, half * (dim // 2) : (half + 1) * (dim // 2)]


def block_kernel(
    n_ref, x_ref, w1_hbm, w2_hbm, out_ref,
    w1, w2, comb, mine, other, acc, hid, y, y_in, z, z_in,
    w1_sem, w2_sem, ps, pr, xs, xr, fs, fr, ys, yr, zs, zr,
):
    tp = lax.axis_index("tp")
    chip, core = tp // 2, tp % 2
    partner = {"tp": chip * 2 + (1 - core)}
    peer = {"tp": (1 - chip) * 2 + core}
    half = n_ref.shape[2]
    width = hid.shape[1]
    rows = out_ref.shape[0]
    nrow, nout = len(ROW_CHUNKS), len(OUT_CHUNKS)

    queue = []
    at = 0
    for j, (start, size) in enumerate(ROW_CHUNKS):
        for side, which in enumerate((core, 1 - core)):
            place = at % W1_ROWS
            queue.append(("w1", size, pltpu.make_async_copy(
                w1_hbm.at[pl.ds(pl.multiple_of(which * half + start, 256), size), :],
                w1.at[pl.ds(place, size), :],
                w1_sem.at[2 * j + side],
            )))
            at += size
    for m, (start, size) in enumerate(OUT_CHUNKS):
        queue.append(("w2", 1, pltpu.make_async_copy(
            w2_hbm.at[:, pl.ds(start, size)],
            w2.at[m % W2_SLOTS, :, pl.ds(0, size)],
            w2_sem.at[m],
        )))
    sizes = [s * width * 2 for _, s in ROW_CHUNKS for _ in range(2)] + [
        s * width * 2 for _, s in OUT_CHUNKS
    ]
    state = {"next": 0, "flight": 0, "w1": W1_ROWS, "w2": W2_SLOTS}

    def pump():
        while state["next"] < len(queue):
            k = state["next"]
            kind, need, copy = queue[k]
            if state[kind] < need or state["flight"] + sizes[k] > IN_FLIGHT:
                break
            copy.start()
            state[kind] -= need
            state["flight"] += sizes[k]
            state["next"] += 1

    def arrived(k):
        queue[k][2].wait()
        state["flight"] -= sizes[k]
        pump()

    def used(k):
        state[queue[k][0]] += queue[k][1]
        pump()

    def part_copy(j):
        cols = pl.ds(*ROW_CHUNKS[j])
        return pltpu.make_async_remote_copy(
            n_ref.at[1 - core, :, cols], comb.at[:, cols], ps.at[j], pr.at[j], partner, MESH
        )

    def peer_copy(j):
        cols = pl.ds(*ROW_CHUNKS[j])
        return pltpu.make_async_remote_copy(
            comb.at[:, cols], mine.at[:, cols], xs.at[j], xr.at[j], peer, MESH
        )

    def full_copy(j):
        cols = pl.ds(*ROW_CHUNKS[j])
        return pltpu.make_async_remote_copy(
            mine.at[:, cols], other.at[:, cols], fs.at[j], fr.at[j], partner, MESH
        )

    def y_copy(m):
        cols = pl.ds(*OUT_CHUNKS[m])
        return pltpu.make_async_remote_copy(
            y.at[1 - core, :, :, cols], y_in.at[:, :, cols], ys.at[m], yr.at[m], partner, MESH
        )

    def z_copy(m):
        cols = pl.ds(*OUT_CHUNKS[m])
        return pltpu.make_async_remote_copy(
            z.at[1 - chip, :, cols], z_in.at[:, cols], zs.at[m], zr.at[m], peer, MESH
        )

    barrier = pltpu.get_barrier_semaphore()
    for who in (partner, peer):
        pl.semaphore_signal(barrier, inc=1, device_id=who, device_id_type=MESH)
    pump()
    pl.semaphore_wait(barrier, 2)

    for j in range(nrow):
        part_copy(j).start()
    for j, (start, size) in enumerate(ROW_CHUNKS):
        cols = pl.ds(start, size)
        part_copy(j).wait_recv()
        comb[:, cols] += n_ref[core, :, cols]
        peer_copy(j).start()

    place = 0
    tile = 512
    for j, (start, size) in enumerate(ROW_CHUNKS):
        cols = pl.ds(start, size)
        peer_copy(j).wait_recv()
        mine[:, cols] += comb[:, cols]
        full_copy(j).start()
        for side, src in enumerate((mine, other)):
            k = 2 * j + side
            if side:
                full_copy(j).wait_recv()
            arrived(k)
            for c in range(0, width, tile):
                part = jnp.dot(
                    src[:, cols], w1[pl.ds(place, size), pl.ds(c, tile)],
                    preferred_element_type=jnp.float32,
                )
                if k > 0:
                    part += acc[:, c : c + tile]
                if k < 2 * nrow - 1:
                    acc[:, c : c + tile] = part
                else:
                    hid[:, c : c + tile] = jax.nn.gelu(
                        part.astype(jnp.bfloat16).astype(jnp.float32), approximate=True
                    ).astype(jnp.bfloat16)
            used(k)
            place = (place + size) % W1_ROWS

    def combine(m):
        cols = pl.ds(*OUT_CHUNKS[m])
        y_copy(m).wait_recv()
        z[:, :, cols] = y[core, :, :, cols] + y_in[:, :, cols]
        z_copy(m).start()

    def finish(m):
        cols = pl.ds(*OUT_CHUNKS[m])
        z_copy(m).wait_recv()
        out_ref[:, cols] = (z[chip, :, cols] + z_in[:, cols]).astype(out_ref.dtype)

    lag, late = 2, 6
    for m in range(nout + late):
        if m < nout:
            start, size = OUT_CHUNKS[m]
            arrived(2 * nrow + m)
            total = x_ref[:, start : start + size].astype(jnp.float32) + jnp.dot(
                hid[...], w2[m % W2_SLOTS, :, :size], preferred_element_type=jnp.float32
            )
            for dest_core in range(2):
                for dest_chip in range(2):
                    at = (dest_chip * 2 + dest_core) * rows
                    y[dest_core, dest_chip, :, start : start + size] = total[at : at + rows]
            y_copy(m).start()
            used(2 * nrow + m)
        if lag <= m < nout + lag:
            combine(m - lag)
        if m >= late:
            finish(m - late)

    for j in range(nrow):
        part_copy(j).wait_send()
        peer_copy(j).wait_send()
        full_copy(j).wait_send()
    for m in range(nout):
        y_copy(m).wait_send()
        z_copy(m).wait_send()


def solution(mesh):
    def device_step(token_ids, table, gain, w_in, w_out):
        tokens = token_ids.shape[0]
        vocab, dim = table.shape
        width = w_in.shape[1]
        half, rows = dim // 2, tokens // 4
        bf16, f32 = jnp.bfloat16, jnp.float32
        dma = pltpu.SemaphoreType.DMA
        vmem = pl.BlockSpec(memory_space=pltpu.VMEM)
        hbm = pl.BlockSpec(memory_space=pl.ANY)
        normed, embedded = pl.pallas_call(
            gather_kernel,
            name="gather_norm",
            out_shape=(
                jax.ShapeDtypeStruct((2, tokens, half), bf16),
                jax.ShapeDtypeStruct((tokens, dim), bf16),
            ),
            in_specs=[hbm, hbm, hbm],
            out_specs=(vmem, vmem),
            scratch_shapes=[
                pltpu.SMEM((tokens,), jnp.int32),
                pltpu.VMEM((dim,), bf16),
                pltpu.VMEM((tokens, SUB, dim), bf16),
                pltpu.VMEM((tokens, 128), jnp.int32),
                dma, dma, dma((tokens,)),
            ],
            compiler_params=pltpu.CompilerParams(vmem_limit_bytes=24 * 2**20),
        )(
            pltpu.with_memory_space_constraint(token_ids, pltpu.HBM),
            table.reshape(vocab // SUB, SUB, dim),
            pltpu.with_memory_space_constraint(gain, pltpu.HBM),
        )

        nrow, nout = len(ROW_CHUNKS), len(OUT_CHUNKS)
        return pl.pallas_call(
            block_kernel,
            name="mlp_block",
            out_shape=jax.ShapeDtypeStruct((rows, dim), bf16),
            in_specs=[vmem, vmem, hbm, hbm],
            out_specs=vmem,
            scratch_shapes=[
                pltpu.VMEM((W1_ROWS, width), bf16),
                pltpu.VMEM((W2_SLOTS, width, 512), bf16),
                pltpu.VMEM((tokens, half), bf16),
                pltpu.VMEM((tokens, half), bf16),
                pltpu.VMEM((tokens, half), bf16),
                pltpu.VMEM((tokens, width), f32),
                pltpu.VMEM((tokens, width), bf16),
                pltpu.VMEM((2, 2, rows, dim), f32),
                pltpu.VMEM((2, rows, dim), f32),
                pltpu.VMEM((2, rows, dim), f32),
                pltpu.VMEM((rows, dim), f32),
                dma((2 * nrow,)), dma((nout,)),
                dma((nrow,)), dma((nrow,)),
                dma((nrow,)), dma((nrow,)),
                dma((nrow,)), dma((nrow,)),
                dma((nout,)), dma((nout,)),
                dma((nout,)), dma((nout,)),
            ],
            compiler_params=pltpu.CompilerParams(
                collective_id=0, has_side_effects=True, vmem_limit_bytes=51 * 2**20
            ),
        )(normed, embedded, w_in, w_out)

    return jax.shard_map(
        device_step,
        mesh=mesh,
        in_specs=(P("dp"), P("tp", None), P(), P(None, "tp"), P("tp", None)),
        out_specs=P(("dp", "tp"), None),
        check_vma=False,
    )
```

time: 95.1 us -> 30.6 us (0.32)
  waiting for transfers between devices: 38.4 us -> 0 us
  Pallas kernels: 0 us -> 29.7 us
  matrix products: 23.1 us -> 0 us
  between operations: 13.4 us -> 0.02 us
  blocking collectives: 9.3 us -> 0 us
  other arithmetic: 6.62 us -> 0 us
  local copies, waits for them, and re-layouts: 3.72 us -> 0.66 us
    reduce_scatter x2 -> x0, waiting for transfers between devices: 38.3 us -> none  [the longest x1 20 us: device_step(): mlp_sum = lax.psum_scatter(mlp_part, 'tp', scatter_dimension=0, tiled=True)]
    pallas_call x0 -> x2, Pallas kernels: none -> 29.7 us  [the longest x1 26 us: device_step(): pl.pallas_call(block_kernel, name='mlp_block', out_shape=jax.ShapeDtypeSt...]
    dot_general x1 -> x0, matrix products: 23.1 us -> none  [device_step(): jnp.dot(activated, w_out_shard, preferred_element_type=jnp.float32)]
    all_gather x1 -> x0, blocking collectives: 9.3 us -> none  [device_step(): normed_all = lax.all_gather(normed, 'tp', axis=0, tiled=True)]
    gather x1 -> x0, local copies, waits for them, and re-layouts: 3.72 us -> none  [device_step(): jnp.take(table_shard, jnp.clip(local_ids, 0, shard_rows - 1), axis=0, mod...]
    convert_element_type x3 -> x0, other arithmetic: 3.34 us -> none  [the longest x1 1.63 us: device_step(): return (embedded.astype(jnp.float32) + mlp_sum).astype(jnp.bfloat16)]
    reduce_sum x1 -> x0, other arithmetic: 1.05 us -> none  [rms_norm(): jnp.mean(rows_f32 * rows_f32, axis=-1, keepdims=True) + RMS_EPS]
  transfers between devices with their start and end apart: 2 -> 0, of which waited for: 2 -> 0; matrix products, arithmetic and copies ran while one was open for 1% -> 0% of each run, Pallas kernels for 0% -> 0%
where the time goes in v2:
time: 30.6 us; the launch traced here: 30.4 us
  Pallas kernels  29.7 us (97%)
  local copies, waits for them, and re-layouts  0.66 us (2%)
    pallas_call x1, Pallas kernels, device_step(): pl.pallas_call(block_kernel, name='mlp_block', out_shape=jax.ShapeDtypeSt...  26 us
    pallas_call x1, Pallas kernels, device_step(): pl.pallas_call(gather_kernel, name='gather_norm', out_shape=(jax.ShapeDty...  3.75 us
    unnamed x1, local copies, waits for them, and re-layouts  0.66 us

profile of v2, /device:TPU:0, one launch (start us, length us, event | category | flops | bytes accessed | tf_op | source)
XLA Modules:
  0.0 30.4 jit_solution(15893222860887363994)
XLA Ops:
  0.0 3.7 %gather_norm.1 = (bf16[2,64,2048]{2,1,0:T(8,128)(2,1)S(1)}, bf16[64,4096]{1,0:T(8,128)(2,1)S(1)}) custom-call(s32[64]{0:T(128)} %ids_hbm.1, bf16[1024,8,4096]{2,1,0:T(8,128)(2,1)} %bitcast.table_ref, bf16[4096]{0:T(1024)(128)(2,1)} %gain_hbm.1), custom_call_target="tpu_custom_call" | custom-call | tf_op jit(solution)/shard_map/gather_norm/pallas_call | solution.py:257
  3.8 26.0 %mlp_block.1 = bf16[16,4096]{1,0:T(8,128)(2,1)S(1)} custom-call(bf16[2,64,2048]{2,1,0:T(8,128)(2,1)S(1)} %get-tuple-element.7.n_ref, bf16[64,4096]{1,0:T(8,128)(2,1)S(1)} %get-tuple-element.8.x_ref, bf16[4096,3584]{1,0:T(8,128)(2,1)} %w1_hbm.1, bf16[3584,4096]{1,0:T(8,128)(2,1)} %w2_hbm.1), custom_call_target="tpu_custom_call" | custom-call | tf_op jit(solution)/shard_map/mlp_block/pallas_call | solution.py:281
  29.7 0.7 %copy.7 = bf16[16,4096]{1,0:T(8,128)(2,1)} copy(bf16[16,4096]{1,0:T(8,128)(2,1)S(1)} %mlp_block.1) | data formatting | bytes 262144

commit v3 on v2

--- a/solution.py
+++ b/solution.py
@@ -7,79 +7,58 @@
 
 RMS_EPS = 1e-6
 MESH = pl.DeviceIdType.MESH
-SUB = 8
+SUB = 2
 
 
 def spans(widths):
     return [(sum(widths[:i]), w) for i, w in enumerate(widths)]
 
 
-ROW_CHUNKS = spans([256, 512, 512, 512, 256])
-OUT_CHUNKS = spans([256] + [512] * 7 + [256])
+ROW_CHUNKS = spans([512] * 4)
+OUT_CHUNKS = spans([512] * 8)
 W1_ROWS = 3072
-W2_SLOTS = 7
-IN_FLIGHT = 22_100_000
-
-
-def gather_kernel(ids_hbm, table_ref, gain_hbm, n_ref, x_ref, ids, gain, buf, tgt, id_sem, g_sem, sem):
-    tokens, dim = x_ref.shape
-    blocks = table_ref.shape[0]
-    first = lax.axis_index("tp") * (blocks * SUB)
+W2_SLOTS = 6
+IN_FLIGHT = 30_000_000
+
+
+def padded_dot(lhs, rhs):
+    rows = lhs.shape[0]
+    both = jnp.concatenate([lhs, lhs], axis=0)
+    return jnp.dot(both, rhs, preferred_element_type=jnp.float32)[:rows]
+
+
+def gather_kernel(ids_hbm, table_ref, gain_hbm, pairs_ref, want_ref, gain_ref, ids, id_sem, g_sem, sem):
+    tokens = ids.shape[0]
+    shard = table_ref.shape[0]
+    tp = lax.axis_index("tp")
     id_copy = pltpu.make_async_copy(ids_hbm, ids, id_sem)
     id_copy.start()
-    gain_copy = pltpu.make_async_copy(gain_hbm, gain, g_sem)
+    gain_copy = pltpu.make_async_copy(gain_hbm, gain_ref, g_sem)
     gain_copy.start()
     id_copy.wait()
 
-    def local(i):
-        at = ids[i] - first
-        return at, (at >= 0) & (at < blocks * SUB)
+    def row_copy(i, at):
+        return pltpu.make_async_copy(
+            table_ref.at[pl.ds(at, SUB), :], pairs_ref.at[pl.ds(i * SUB, SUB), :], sem.at[i]
+        )
 
     for i in range(tokens):
-        at, owned = local(i)
-
-        @pl.when(owned)
-        def _():
-            pltpu.make_async_copy(
-                table_ref.at[lax.shift_right_logical(at, 3)], buf.at[i], sem.at[i]
-            ).start()
-
+        pair = ids[i] & (shard - SUB)
+        row_copy(i, pl.multiple_of(pair, SUB)).start()
     for i in range(tokens):
-        at, owned = local(i)
-
-        @pl.when(jnp.logical_not(owned))
-        def _():
-            buf[i] = jnp.zeros(buf.shape[1:], buf.dtype)
-
-        tgt[i, :] = jnp.full((128,), jnp.where(owned, i * SUB + (at & (SUB - 1)), -1), jnp.int32)
-
-    lane = lax.broadcasted_iota(jnp.int32, (tokens, 128), 1)
-    want = tgt[...]
-    pick = jnp.concatenate(
-        [jnp.where(lane + 128 * b == want, 1.0, 0.0) for b in range(tokens * SUB // 128)], axis=1
-    ).astype(jnp.bfloat16)
+        at = ids[i] - tp * shard
+        owned = (at >= 0) & (at < shard)
+        want_ref[i, :] = jnp.full(
+            (128,), jnp.where(owned, i * SUB + (at & (SUB - 1)), -1), jnp.int32
+        )
     gain_copy.wait()
     for i in range(tokens):
-        at, owned = local(i)
-
-        @pl.when(owned)
-        def _():
-            pltpu.make_async_copy(table_ref.at[0], buf.at[i], sem.at[i]).wait()
-
-    rows = jnp.dot(
-        pick, buf[...].reshape(tokens * SUB, dim), preferred_element_type=jnp.float32
-    )
-    x_ref[...] = rows.astype(jnp.bfloat16)
-    inv_rms = lax.rsqrt(jnp.mean(rows * rows, axis=-1, keepdims=True) + RMS_EPS)
-    scale = gain[...].astype(jnp.float32).reshape(1, dim)
-    normed = (rows * inv_rms * scale).astype(jnp.bfloat16)
-    for half in range(2):
-        n_ref[half] = normed[:, half * (dim // 2) : (half + 1) * (dim // 2)]
+        row_copy(i, 0).wait()
 
 
 def block_kernel(
-    n_ref, x_ref, w1_hbm, w2_hbm, out_ref,
-    w1, w2, comb, mine, other, acc, hid, y, y_in, z, z_in,
+    pairs_ref, want_ref, gain_ref, w1_hbm, w2_hbm, out_ref,
+    n_ref, x_ref, w1, w2, comb, mine, other, acc, hid, y, y_in, z, z_in,
     w1_sem, w2_sem, ps, pr, xs, xr, fs, fr, ys, yr, zs, zr,
 ):
     tp = lax.axis_index("tp")
@@ -93,9 +72,10 @@
 
     queue = []
     at = 0
+    places = {}
     for j, (start, size) in enumerate(ROW_CHUNKS):
         for side, which in enumerate((core, 1 - core)):
-            place = at % W1_ROWS
+            place = places[j, side] = at % W1_ROWS
             queue.append(("w1", size, pltpu.make_async_copy(
                 w1_hbm.at[pl.ds(pl.multiple_of(which * half + start, 256), size), :],
                 w1.at[pl.ds(place, size), :],
@@ -167,6 +147,25 @@
     for who in (partner, peer):
         pl.semaphore_signal(barrier, inc=1, device_id=who, device_id_type=MESH)
     pump()
+
+    tokens, dim = x_ref.shape
+    lane = lax.broadcasted_iota(jnp.int32, (tokens, 128), 1)
+    want = want_ref[...]
+    pick = jnp.concatenate(
+        [jnp.where(lane + 128 * b == want, 1.0, 0.0) for b in range(tokens * SUB // 128)], axis=1
+    ).astype(jnp.bfloat16)
+    tile = 512
+    squares = jnp.zeros((tokens, 1), jnp.float32)
+    for c in range(0, dim, tile):
+        picked = padded_dot(pick, pairs_ref[:, c : c + tile])
+        squares += jnp.sum(picked * picked, axis=-1, keepdims=True)
+        x_ref[:, c : c + tile] = picked.astype(jnp.bfloat16)
+    inv_rms = lax.rsqrt(squares / dim + RMS_EPS)
+    for c in range(0, dim, tile):
+        scale = gain_ref[c : c + tile].astype(jnp.float32).reshape(1, tile)
+        n_ref[c // half, :, c % half : c % half + tile] = (
+            x_ref[:, c : c + tile].astype(jnp.float32) * inv_rms * scale
+        ).astype(jnp.bfloat16)
     pl.semaphore_wait(barrier, 2)
 
     for j in range(nrow):
@@ -177,33 +176,35 @@
         comb[:, cols] += n_ref[core, :, cols]
         peer_copy(j).start()
 
-    place = 0
-    tile = 512
+    def rows_dot(j, side):
+        start, size = ROW_CHUNKS[j]
+        cols = pl.ds(start, size)
+        src = (mine, other)[side]
+        if side:
+            full_copy(j).wait_recv()
+        arrived(2 * j + side)
+        held = w1.at[pl.ds(places[j, side], size), :]
+        for c in range(0, width, tile):
+            part = padded_dot(src[:, cols], held[:, pl.ds(c, tile)])
+            if (j, side) != (0, 0):
+                part += acc[:, c : c + tile]
+            if (j, side) != (nrow - 1, 1):
+                acc[:, c : c + tile] = part
+            else:
+                hid[:, c : c + tile] = jax.nn.gelu(
+                    part.astype(jnp.bfloat16).astype(jnp.float32), approximate=True
+                ).astype(jnp.bfloat16)
+        used(2 * j + side)
+
     for j, (start, size) in enumerate(ROW_CHUNKS):
         cols = pl.ds(start, size)
         peer_copy(j).wait_recv()
         mine[:, cols] += comb[:, cols]
         full_copy(j).start()
-        for side, src in enumerate((mine, other)):
-            k = 2 * j + side
-            if side:
-                full_copy(j).wait_recv()
-            arrived(k)
-            for c in range(0, width, tile):
-                part = jnp.dot(
-                    src[:, cols], w1[pl.ds(place, size), pl.ds(c, tile)],
-                    preferred_element_type=jnp.float32,
-                )
-                if k > 0:
-                    part += acc[:, c : c + tile]
-                if k < 2 * nrow - 1:
-                    acc[:, c : c + tile] = part
-                else:
-                    hid[:, c : c + tile] = jax.nn.gelu(
-                        part.astype(jnp.bfloat16).astype(jnp.float32), approximate=True
-                    ).astype(jnp.bfloat16)
-            used(k)
-            place = (place + size) % W1_ROWS
+        if j:
+            rows_dot(j - 1, 1)
+        rows_dot(j, 0)
+    rows_dot(nrow - 1, 1)
 
     def combine(m):
         cols = pl.ds(*OUT_CHUNKS[m])
@@ -221,8 +222,8 @@
         if m < nout:
             start, size = OUT_CHUNKS[m]
             arrived(2 * nrow + m)
-            total = x_ref[:, start : start + size].astype(jnp.float32) + jnp.dot(
-                hid[...], w2[m % W2_SLOTS, :, :size], preferred_element_type=jnp.float32
+            total = x_ref[:, start : start + size].astype(jnp.float32) + padded_dot(
+                hid[...], w2[m % W2_SLOTS, :, :size]
             )
             for dest_core in range(2):
                 for dest_chip in range(2):
@@ -247,33 +248,28 @@
 def solution(mesh):
     def device_step(token_ids, table, gain, w_in, w_out):
         tokens = token_ids.shape[0]
-        vocab, dim = table.shape
+        dim = table.shape[1]
         width = w_in.shape[1]
         half, rows = dim // 2, tokens // 4
         bf16, f32 = jnp.bfloat16, jnp.float32
         dma = pltpu.SemaphoreType.DMA
         vmem = pl.BlockSpec(memory_space=pltpu.VMEM)
         hbm = pl.BlockSpec(memory_space=pl.ANY)
-        normed, embedded = pl.pallas_call(
+        pairs, want, gains = pl.pallas_call(
             gather_kernel,
-            name="gather_norm",
+            name="gather_rows",
             out_shape=(
-                jax.ShapeDtypeStruct((2, tokens, half), bf16),
-                jax.ShapeDtypeStruct((tokens, dim), bf16),
+                jax.ShapeDtypeStruct((tokens * SUB, dim), bf16),
+                jax.ShapeDtypeStruct((tokens, 128), jnp.int32),
+                jax.ShapeDtypeStruct((dim,), bf16),
             ),
             in_specs=[hbm, hbm, hbm],
-            out_specs=(vmem, vmem),
-            scratch_shapes=[
-                pltpu.SMEM((tokens,), jnp.int32),
-                pltpu.VMEM((dim,), bf16),
-                pltpu.VMEM((tokens, SUB, dim), bf16),
-                pltpu.VMEM((tokens, 128), jnp.int32),
-                dma, dma, dma((tokens,)),
-            ],
-            compiler_params=pltpu.CompilerParams(vmem_limit_bytes=24 * 2**20),
+            out_specs=(vmem, vmem, vmem),
+            scratch_shapes=[pltpu.SMEM((tokens,), jnp.int32), dma, dma, dma((tokens,))],
+            compiler_params=pltpu.CompilerParams(vmem_limit_bytes=16 * 2**20),
         )(
             pltpu.with_memory_space_constraint(token_ids, pltpu.HBM),
-            table.reshape(vocab // SUB, SUB, dim),
+            table,
             pltpu.with_memory_space_constraint(gain, pltpu.HBM),
         )
 
@@ -282,9 +278,11 @@
             block_kernel,
             name="mlp_block",
             out_shape=jax.ShapeDtypeStruct((rows, dim), bf16),
-            in_specs=[vmem, vmem, hbm, hbm],
+            in_specs=[vmem, vmem, vmem, hbm, hbm],
             out_specs=vmem,
             scratch_shapes=[
+                pltpu.VMEM((2, tokens, half), bf16),
+                pltpu.VMEM((tokens, dim), bf16),
                 pltpu.VMEM((W1_ROWS, width), bf16),
                 pltpu.VMEM((W2_SLOTS, width, 512), bf16),
                 pltpu.VMEM((tokens, half), bf16),
@@ -304,9 +302,9 @@
                 dma((nout,)), dma((nout,)),
             ],
             compiler_params=pltpu.CompilerParams(
-                collective_id=0, has_side_effects=True, vmem_limit_bytes=51 * 2**20
+                collective_id=0, has_side_effects=True, vmem_limit_bytes=49 * 2**20
             ),
-        )(normed, embedded, w_in, w_out)
+        )(pairs, want, gains, w_in, w_out)
 
     return jax.shard_map(
         device_step,

time: 30.6 us -> 29.5 us (0.964)
  Pallas kernels: 29.7 us -> 28.6 us
    pallas_call x1, Pallas kernels: 3.75 us -> 2.44 us  [device_step(): pl.pallas_call(gather_kernel, name='gather_rows', out_shape=(jax.ShapeDty...]
where the time goes in v3:
time: 29.5 us; the launch traced here: 29.3 us
  Pallas kernels  28.6 us (97%)
  local copies, waits for them, and re-layouts  0.66 us (2%)
    pallas_call x1, Pallas kernels, device_step(): pl.pallas_call(block_kernel, name='mlp_block', out_shape=jax.ShapeDtypeSt...  26.2 us
    pallas_call x1, Pallas kernels, device_step(): pl.pallas_call(gather_kernel, name='gather_rows', out_shape=(jax.ShapeDty...  2.44 us
    unnamed x1, local copies, waits for them, and re-layouts  0.66 us

profile of v3, /device:TPU:0, one launch (start us, length us, event | category | flops | bytes accessed | tf_op | source)
XLA Modules:
  0.0 29.3 jit_solution(2252305020875081467)
XLA Ops:
  0.0 2.4 %gather_rows.1 = (bf16[128,4096]{1,0:T(8,128)(2,1)S(1)}, s32[64,128]{1,0:T(8,128)S(1)}, bf16[4096]{0:T(1024)(128)(2,1)S(1)}) custom-call(s32[64]{0:T(128)} %ids_hbm.1, bf16[8192,4096]{1,0:T(8,128)(2,1)} %table_ref.1, bf16[4096]{0:T(1024)(128)(2,1)} %gain_hbm.1), custom_call_target="tpu_custom_call" | custom-call | tf_op jit(solution)/shard_map/gather_rows/pallas_call | solution.py:258
  2.5 26.2 %mlp_block.1 = bf16[16,4096]{1,0:T(8,128)(2,1)S(1)} custom-call(bf16[128,4096]{1,0:T(8,128)(2,1)S(1)} %get-tuple-element.8.pairs_ref, s32[64,128]{1,0:T(8,128)S(1)} %get-tuple-element.9.want_ref, bf16[4096]{0:T(1024)(128)(2,1)S(1)} %get-tuple-element.10.gain_ref, bf16[4096,3584]{1,0:T(8,128)(2,1)} %w1_hbm.1, bf16[3584,4096]{1,0:T(8,128)(2,1)} %w2_hbm.1), custom_call_target="tpu_custom_call" | custom-call | tf_op jit(solution)/shard_map/mlp_block/pallas_call | solution.py:277
  28.7 0.7 %copy.7 = bf16[16,4096]{1,0:T(8,128)(2,1)} copy(bf16[16,4096]{1,0:T(8,128)(2,1)S(1)} %mlp_block.1) | data formatting | bytes 262144

commit v4 on v3

--- a/solution.py
+++ b/solution.py
@@ -15,10 +15,10 @@
 
 
 ROW_CHUNKS = spans([512] * 4)
-OUT_CHUNKS = spans([512] * 8)
-W1_ROWS = 3072
-W2_SLOTS = 6
-IN_FLIGHT = 30_000_000
+OUT_CHUNKS = spans([512] * 7 + [256] * 2)
+W1_ROWS = 3584
+W2_SLOTS = 5
+IN_FLIGHT = 34_000_000
 
 
 def padded_dot(lhs, rhs):
@@ -27,7 +27,10 @@
     return jnp.dot(both, rhs, preferred_element_type=jnp.float32)[:rows]
 
 
-def gather_kernel(ids_hbm, table_ref, gain_hbm, pairs_ref, want_ref, gain_ref, ids, id_sem, g_sem, sem):
+def gather_kernel(
+    ids_hbm, table_ref, gain_hbm, w1_hbm, pairs_ref, want_ref, gain_ref, early_ref,
+    ids, id_sem, g_sem, sem, w_sem,
+):
     tokens = ids.shape[0]
     shard = table_ref.shape[0]
     tp = lax.axis_index("tp")
@@ -35,6 +38,11 @@
     id_copy.start()
     gain_copy = pltpu.make_async_copy(gain_hbm, gain_ref, g_sem)
     gain_copy.start()
+    first = (tp % 2) * (pairs_ref.shape[1] // 2)
+    early_copy = pltpu.make_async_copy(
+        w1_hbm.at[pl.ds(pl.multiple_of(first, 512), early_ref.shape[0]), :], early_ref, w_sem
+    )
+    early_copy.start()
     id_copy.wait()
 
     def row_copy(i, at):
@@ -54,10 +62,11 @@
     gain_copy.wait()
     for i in range(tokens):
         row_copy(i, 0).wait()
+    early_copy.wait()
 
 
 def block_kernel(
-    pairs_ref, want_ref, gain_ref, w1_hbm, w2_hbm, out_ref,
+    pairs_ref, want_ref, gain_ref, early_ref, w1_hbm, w2_hbm, out_ref,
     n_ref, x_ref, w1, w2, comb, mine, other, acc, hid, y, y_in, z, z_in,
     w1_sem, w2_sem, ps, pr, xs, xr, fs, fr, ys, yr, zs, zr,
 ):
@@ -75,6 +84,8 @@
     places = {}
     for j, (start, size) in enumerate(ROW_CHUNKS):
         for side, which in enumerate((core, 1 - core)):
+            if (j, side) == (0, 0):
+                continue
             place = places[j, side] = at % W1_ROWS
             queue.append(("w1", size, pltpu.make_async_copy(
                 w1_hbm.at[pl.ds(pl.multiple_of(which * half + start, 256), size), :],
@@ -88,7 +99,7 @@
             w2.at[m % W2_SLOTS, :, pl.ds(0, size)],
             w2_sem.at[m],
         )))
-    sizes = [s * width * 2 for _, s in ROW_CHUNKS for _ in range(2)] + [
+    sizes = [s * width * 2 for _, s in ROW_CHUNKS for _ in range(2)][1:] + [
         s * width * 2 for _, s in OUT_CHUNKS
     ]
     state = {"next": 0, "flight": 0, "w1": W1_ROWS, "w2": W2_SLOTS}
@@ -155,21 +166,27 @@
         [jnp.where(lane + 128 * b == want, 1.0, 0.0) for b in range(tokens * SUB // 128)], axis=1
     ).astype(jnp.bfloat16)
     tile = 512
-    squares = jnp.zeros((tokens, 1), jnp.float32)
+    squares = jnp.zeros((tokens, 128), jnp.float32)
     for c in range(0, dim, tile):
         picked = padded_dot(pick, pairs_ref[:, c : c + tile])
-        squares += jnp.sum(picked * picked, axis=-1, keepdims=True)
+        for lanes in range(0, tile, 128):
+            squares += picked[:, lanes : lanes + 128] * picked[:, lanes : lanes + 128]
         x_ref[:, c : c + tile] = picked.astype(jnp.bfloat16)
-    inv_rms = lax.rsqrt(squares / dim + RMS_EPS)
-    for c in range(0, dim, tile):
-        scale = gain_ref[c : c + tile].astype(jnp.float32).reshape(1, tile)
-        n_ref[c // half, :, c % half : c % half + tile] = (
-            x_ref[:, c : c + tile].astype(jnp.float32) * inv_rms * scale
+    inv_rms = lax.rsqrt(jnp.sum(squares, axis=-1, keepdims=True) / dim + RMS_EPS)
+
+    def normalize(side, start, size):
+        at = pl.ds(pl.multiple_of(side * half + start, 128), size)
+        scale = gain_ref[at].astype(jnp.float32).reshape(1, size)
+        n_ref[side, :, start : start + size] = (
+            x_ref[:, at].astype(jnp.float32) * inv_rms * scale
         ).astype(jnp.bfloat16)
+
     pl.semaphore_wait(barrier, 2)
-
-    for j in range(nrow):
+    for j, (start, size) in enumerate(ROW_CHUNKS):
+        normalize(1 - core, start, size)
         part_copy(j).start()
+    for start, size in ROW_CHUNKS:
+        normalize(core, start, size)
     for j, (start, size) in enumerate(ROW_CHUNKS):
         cols = pl.ds(start, size)
         part_copy(j).wait_recv()
@@ -182,8 +199,11 @@
         src = (mine, other)[side]
         if side:
             full_copy(j).wait_recv()
-        arrived(2 * j + side)
-        held = w1.at[pl.ds(places[j, side], size), :]
+        if (j, side) == (0, 0):
+            held = early_ref
+        else:
+            arrived(2 * j + side - 1)
+            held = w1.at[pl.ds(places[j, side], size), :]
         for c in range(0, width, tile):
             part = padded_dot(src[:, cols], held[:, pl.ds(c, tile)])
             if (j, side) != (0, 0):
@@ -194,7 +214,8 @@
                 hid[:, c : c + tile] = jax.nn.gelu(
                     part.astype(jnp.bfloat16).astype(jnp.float32), approximate=True
                 ).astype(jnp.bfloat16)
-        used(2 * j + side)
+        if (j, side) != (0, 0):
+            used(2 * j + side - 1)
 
     for j, (start, size) in enumerate(ROW_CHUNKS):
         cols = pl.ds(start, size)
@@ -221,7 +242,7 @@
     for m in range(nout + late):
         if m < nout:
             start, size = OUT_CHUNKS[m]
-            arrived(2 * nrow + m)
+            arrived(2 * nrow - 1 + m)
             total = x_ref[:, start : start + size].astype(jnp.float32) + padded_dot(
                 hid[...], w2[m % W2_SLOTS, :, :size]
             )
@@ -230,7 +251,7 @@
                     at = (dest_chip * 2 + dest_core) * rows
                     y[dest_core, dest_chip, :, start : start + size] = total[at : at + rows]
             y_copy(m).start()
-            used(2 * nrow + m)
+            used(2 * nrow - 1 + m)
         if lag <= m < nout + lag:
             combine(m - lag)
         if m >= late:
@@ -255,22 +276,24 @@
         dma = pltpu.SemaphoreType.DMA
         vmem = pl.BlockSpec(memory_space=pltpu.VMEM)
         hbm = pl.BlockSpec(memory_space=pl.ANY)
-        pairs, want, gains = pl.pallas_call(
+        pairs, want, gains, early = pl.pallas_call(
             gather_kernel,
             name="gather_rows",
             out_shape=(
                 jax.ShapeDtypeStruct((tokens * SUB, dim), bf16),
                 jax.ShapeDtypeStruct((tokens, 128), jnp.int32),
                 jax.ShapeDtypeStruct((dim,), bf16),
+                jax.ShapeDtypeStruct((ROW_CHUNKS[0][1], width), bf16),
             ),
-            in_specs=[hbm, hbm, hbm],
-            out_specs=(vmem, vmem, vmem),
-            scratch_shapes=[pltpu.SMEM((tokens,), jnp.int32), dma, dma, dma((tokens,))],
+            in_specs=[hbm, hbm, hbm, hbm],
+            out_specs=(vmem, vmem, vmem, vmem),
+            scratch_shapes=[pltpu.SMEM((tokens,), jnp.int32), dma, dma, dma((tokens,)), dma],
             compiler_params=pltpu.CompilerParams(vmem_limit_bytes=16 * 2**20),
         )(
             pltpu.with_memory_space_constraint(token_ids, pltpu.HBM),
             table,
             pltpu.with_memory_space_constraint(gain, pltpu.HBM),
+            pltpu.with_memory_space_constraint(w_in, pltpu.HBM),
         )
 
         nrow, nout = len(ROW_CHUNKS), len(OUT_CHUNKS)
@@ -278,7 +301,7 @@
             block_kernel,
             name="mlp_block",
             out_shape=jax.ShapeDtypeStruct((rows, dim), bf16),
-            in_specs=[vmem, vmem, vmem, hbm, hbm],
+            in_specs=[vmem, vmem, vmem, vmem, hbm, hbm],
             out_specs=vmem,
             scratch_shapes=[
                 pltpu.VMEM((2, tokens, half), bf16),
@@ -302,9 +325,9 @@
                 dma((nout,)), dma((nout,)),
             ],
             compiler_params=pltpu.CompilerParams(
-                collective_id=0, has_side_effects=True, vmem_limit_bytes=49 * 2**20
+                collective_id=0, has_side_effects=True, vmem_limit_bytes=97 * 2**19
             ),
-        )(pairs, want, gains, w_in, w_out)
+        )(pairs, want, gains, early, w_in, w_out)
 
     return jax.shard_map(
         device_step,

time: 29.5 us -> 28.7 us (0.973)
  Pallas kernels: 28.6 us -> 27.9 us
    pallas_call x1, Pallas kernels: 26.2 us -> 24.9 us  [device_step(): pl.pallas_call(block_kernel, name='mlp_block', out_shape=jax.ShapeDtypeSt...]
    pallas_call x1, Pallas kernels: 2.44 us -> 3.02 us  [device_step(): pl.pallas_call(gather_kernel, name='gather_rows', out_shape=(jax.ShapeDty...]
where the time goes in v4:
time: 28.7 us; the launch traced here: 28.6 us
  Pallas kernels  27.9 us (97%)
  local copies, waits for them, and re-layouts  0.66 us (2%)
    pallas_call x1, Pallas kernels, device_step(): pl.pallas_call(block_kernel, name='mlp_block', out_shape=jax.ShapeDtypeSt...  24.9 us
    pallas_call x1, Pallas kernels, device_step(): pl.pallas_call(gather_kernel, name='gather_rows', out_shape=(jax.ShapeDty...  3.02 us
    unnamed x1, local copies, waits for them, and re-layouts  0.66 us

profile of v4, /device:TPU:0, one launch (start us, length us, event | category | flops | bytes accessed | tf_op | source)
XLA Modules:
  0.0 28.6 jit_solution(6512254232254219740)
XLA Ops:
  0.0 3.0 %gather_rows.1 = (bf16[128,4096]{1,0:T(8,128)(2,1)S(1)}, s32[64,128]{1,0:T(8,128)S(1)}, bf16[4096]{0:T(1024)(128)(2,1)S(1)}, bf16[512,3584]{1,0:T(8,128)(2,1)S(1)}) custom-call(s32[64]{0:T(128)} %ids_hbm.1, bf16[8192,4096]{1,0:T(8,128)(2,1)} %table_ref.1, bf16[4096]{0:T(1024)(128)(2,1)} %gain_hbm.1, bf16[4096,3584]{1,0:T(8,128)(2,1)} %w1_hbm.3), custom_call_target="tpu_custom_call" | custom-call | tf_op jit(solution)/shard_map/gather_rows/pallas_call | solution.py:279
  3.0 24.9 %mlp_block.1 = bf16[16,4096]{1,0:T(8,128)(2,1)S(1)} custom-call(bf16[128,4096]{1,0:T(8,128)(2,1)S(1)} %get-tuple-element.9.pairs_ref, s32[64,128]{1,0:T(8,128)S(1)} %get-tuple-element.10.want_ref, bf16[4096]{0:T(1024)(128)(2,1)S(1)} %get-tuple-element.11.gain_ref, bf16[512,3584]{1,0:T(8,128)(2,1)S(1)} %get-tuple-element.12.early_ref, ...), custom_call_target="tpu_custom_call" | custom-call | tf_op jit(solution)/shard_map/mlp_block/pallas_call | solution.py:300
  27.9 0.7 %copy.7 = bf16[16,4096]{1,0:T(8,128)(2,1)} copy(bf16[16,4096]{1,0:T(8,128)(2,1)S(1)} %mlp_block.1) | data formatting | bytes 262144

commit v5 on v4

--- a/solution.py
+++ b/solution.py
@@ -168,7 +168,9 @@
     tile = 512
     squares = jnp.zeros((tokens, 128), jnp.float32)
     for c in range(0, dim, tile):
-        picked = padded_dot(pick, pairs_ref[:, c : c + tile])
+        picked = jnp.dot(
+            pick, pairs_ref[:, c : c + tile], preferred_element_type=jnp.float32
+        )
         for lanes in range(0, tile, 128):
             squares += picked[:, lanes : lanes + 128] * picked[:, lanes : lanes + 128]
         x_ref[:, c : c + tile] = picked.astype(jnp.bfloat16)
@@ -203,6 +205,8 @@
             held = early_ref
         else:
             arrived(2 * j + side - 1)
+            if (j, side) == (nrow - 1, 1):
+                arrived(2 * nrow - 1)
             held = w1.at[pl.ds(places[j, side], size), :]
         for c in range(0, width, tile):
             part = padded_dot(src[:, cols], held[:, pl.ds(c, tile)])
@@ -242,7 +246,8 @@
     for m in range(nout + late):
         if m < nout:
             start, size = OUT_CHUNKS[m]
-            arrived(2 * nrow - 1 + m)
+            if m > 0:
+                arrived(2 * nrow - 1 + m)
             total = x_ref[:, start : start + size].astype(jnp.float32) + padded_dot(
                 hid[...], w2[m % W2_SLOTS, :, :size]
             )

time: 28.7 us -> 28.6 us (level)
  no operation moved by 1% of the time
where the time goes in v5:
time: 28.6 us; the launch traced here: 28.5 us
  Pallas kernels  27.8 us (97%)
  local copies, waits for them, and re-layouts  0.66 us (2%)
    pallas_call x1, Pallas kernels, device_step(): pl.pallas_call(block_kernel, name='mlp_block', out_shape=jax.ShapeDtypeSt...  24.8 us
    pallas_call x1, Pallas kernels, device_step(): pl.pallas_call(gather_kernel, name='gather_rows', out_shape=(jax.ShapeDty...  3.02 us
    unnamed x1, local copies, waits for them, and re-layouts  0.66 us

profile of v5, /device:TPU:0, one launch (start us, length us, event | category | flops | bytes accessed | tf_op | source)
XLA Modules:
  0.0 28.5 jit_solution(9973522507443342926)
XLA Ops:
  0.0 3.0 %gather_rows.1 = (bf16[128,4096]{1,0:T(8,128)(2,1)S(1)}, s32[64,128]{1,0:T(8,128)S(1)}, bf16[4096]{0:T(1024)(128)(2,1)S(1)}, bf16[512,3584]{1,0:T(8,128)(2,1)S(1)}) custom-call(s32[64]{0:T(128)} %ids_hbm.1, bf16[8192,4096]{1,0:T(8,128)(2,1)} %table_ref.1, bf16[4096]{0:T(1024)(128)(2,1)} %gain_hbm.1, bf16[4096,3584]{1,0:T(8,128)(2,1)} %w1_hbm.3), custom_call_target="tpu_custom_call" | custom-call | tf_op jit(solution)/shard_map/gather_rows/pallas_call | solution.py:284
  3.0 24.8 %mlp_block.1 = bf16[16,4096]{1,0:T(8,128)(2,1)S(1)} custom-call(bf16[128,4096]{1,0:T(8,128)(2,1)S(1)} %get-tuple-element.9.pairs_ref, s32[64,128]{1,0:T(8,128)S(1)} %get-tuple-element.10.want_ref, bf16[4096]{0:T(1024)(128)(2,1)S(1)} %get-tuple-element.11.gain_ref, bf16[512,3584]{1,0:T(8,128)(2,1)S(1)} %get-tuple-element.12.early_ref, ...), custom_call_target="tpu_custom_call" | custom-call | tf_op jit(solution)/shard_map/mlp_block/pallas_call | solution.py:305
  27.8 0.7 %copy.7 = bf16[16,4096]{1,0:T(8,128)(2,1)} copy(bf16[16,4096]{1,0:T(8,128)(2,1)S(1)} %mlp_block.1) | data formatting | bytes 262144
